TPU v7x, 32 devices: a whole 2x2x4 slice. The times are simulated.
32 devices in a mesh: cols: 8 (over y, x, core), rows: 4 (over z).
Axes of the slice: x: 2, y: 2, z: 4, core: 2. Of those that a mesh axis runs over, the one named last changes fastest.
Arguments:
- weight: float32 [8192, 28672], P('rows', 'cols'), may hold values from -6 to 6
- scales: float32 [8192], P('rows'), may hold values from 0.2 to 0.5
- panels: float32 [1024, 28672], P('cols', 'rows')
- block_inverse: float32 [2, 128, 128], replicated
- grid_codes: int32 [16], replicated, may hold values from -12 to 12, as said below
- block_starts: int32 [2], replicated, may hold values from 0 to 25088, as said below
Outputs:
- result: float32 [8192, 28672], P('rows', 'cols')
Inputs may be any that keep to these rules, and one draw needn't show every extreme that they name: `grid_codes`: strictly increasing. `block_starts`: strictly increasing multiples of 3584; the last block starts at the last device's columns.
All inputs are finite; a program needn't handle non-finite values.
Results may differ from a plain program's by a relative error of at most 0.00012.
Values sent between devices are 32-bit elements; how exact they have to be, the bound alone decides.
A program may use at most 192 MiB of HBM per device.

v0:
```python
import jax
import jax.numpy as jnp
from jax import lax
from jax.sharding import PartitionSpec as P

BLK = 128
SUB = 32
LEVELS = 16
BLOCKS = 2


softness = 0.2


def from_root(value, axis, source):
    kept = jnp.where(lax.axis_index(axis) == source, value, 0).astype(value.dtype)
    return lax.psum(kept, axis)


def quantize(values, scales, grid_codes):
    levels = grid_codes.astype(jnp.float32)
    ratio = values / scales[:, None]
    output = jnp.zeros_like(values) + levels[0]
    for level_id in range(LEVELS - 1):
        level_gap = levels[level_id + 1] - levels[level_id]
        midpoint = 0.5 * (levels[level_id] + levels[level_id + 1])
        output = output + level_gap * jax.nn.sigmoid((ratio - midpoint) / softness)
    return output * scales[:, None]


def inner_block(block_cols, diag_block, inverse, scales, grid_codes):
    local_ids = jnp.arange(BLK, dtype=jnp.int32)
    pieces = []
    for piece_id in range(BLK // SUB):
        low_col = piece_id * SUB
        current = block_cols[:, low_col : low_col + SUB]
        quantized = quantize(current, scales, grid_codes)
        error_part = jnp.dot(
            current - quantized,
            inverse[low_col : low_col + SUB, low_col : low_col + SUB],
            precision=lax.Precision.HIGHEST,
            preferred_element_type=jnp.float32,
        )
        later_rows = jnp.where(
            local_ids[None, :] >= low_col + SUB, diag_block[low_col : low_col + SUB, :], 0.0
        )
        block_cols = block_cols - jnp.dot(
            error_part,
            later_rows,
            precision=lax.Precision.HIGHEST,
            preferred_element_type=jnp.float32,
        )
        block_cols = block_cols.at[:, low_col : low_col + SUB].set(quantized)
        pieces.append(error_part)
    return (block_cols, jnp.concatenate(pieces, axis=1))


def local(weight, scales, panels, block_inverse, grid_codes, block_starts):
    cols_per = weight.shape[1]
    slab_width = panels.shape[1]
    own_index = lax.axis_index("cols")
    first_col = own_index * cols_per
    column_ids = first_col + jnp.arange(cols_per, dtype=jnp.int32)
    holder = first_col // slab_width
    offset = first_col - holder * slab_width
    for block_id in range(BLOCKS):
        start_col = block_starts[block_id]
        owner_id = start_col // cols_per
        panel_slab = from_root(panels, "cols", owner_id)
        needed = lax.dynamic_slice_in_dim(panel_slab, offset, cols_per, 1)
        panel_local = from_root(needed, "rows", holder)
        trail_rows = jnp.where(column_ids[None, :] >= start_col + BLK, panel_local, 0.0)
        diag_block, trail_rows = (panel_local[:, :BLK], trail_rows)
        block_cols, errors = inner_block(
            weight[:, :BLK], diag_block, block_inverse[block_id], scales, grid_codes
        )
        errors = from_root(errors, "cols", owner_id)
        block_cols, errors = (block_cols, errors)
        weight = jnp.where(own_index == owner_id, weight.at[:, :BLK].set(block_cols), weight)
        weight = weight - jnp.dot(
            errors, trail_rows, precision=lax.Precision.HIGHEST, preferred_element_type=jnp.float32
        )
    return weight


def solution(mesh):
    placed = (P("rows", "cols"), P("rows"), P("cols", "rows"), P(), P(), P())
    return jax.shard_map(
        local, mesh=mesh, in_specs=placed, out_specs=P("rows", "cols"), check_vma=False
    )
```

profile of v0, /device:TPU:7, one launch (start us, length us, event | category | flops | bytes accessed | tf_op | source)
XLA Modules:
  0.0 511.5 jit_solution(3823678485679599117)
XLA Ops:
  11.7 5.9 %broadcast_select_fusion = (f32[128,7168]{1,0:T(8,128)}, f32[128,7168]{1,0:T(8,128)}) fusion(f32[128,7168]{1,0:T(8,128)} %param.28, pred[]{:T(512)S(6)} %eq.16, pred[]{:T(512)S(6)} %eq.6), kind=kLoop, calls=%fused_computation.14 | loop fusion | flops 1835008 | bytes 11010050 | tf_op jit(solution)/shard_map/jit(_where)/select_n | solution.py:16
  17.7 75.3 %all-reduce.7.cloned.1.call-done = f32[128,7168]{1,0:T(8,128)} async-done(((f32[128,7168]{1,0:T(8,128)}), f32[128,7168]{1,0:T(8,128)}) %all-reduce.7.cloned.1.call-update) | async-done | bytes 3670032 | tf_op jit(solution)/shard_map/psum | solution.py:17
  93.1 2.9 dynamic-slice_select_fusion.1
  135.1 29.9 %copy.9 = f32[2048,3584]{0,1:T(8,128)} copy(f32[2048,3584]{1,0:T(8,128)} %param.26) | data formatting | bytes 58720256 | tf_op args[0]
  166.4 3.1 fusion.28
  169.5 4.2 all-reduce.9.cloned.1.call-done
  173.7 2.3 convolution_subtract_fusion.9
  176.1 3.2 fusion.13
  179.3 2.1 fusion.26
  182.5 2.3 fusion.12
  184.8 2.0 fusion.24
  187.9 2.3 fusion.11
  190.3 14.5 %fusion.22 = f32[2048,32]{0,1:T(8,128)S(1)} fusion(f32[2048,128]{0,1:T(8,128)S(1)} %fusion.11, f32[128,128]{1,0:T(8,128)S(1)} %get-tuple-element.130, f32[]{:T(128)S(6)} %mul.363, f32[]{:T(128)S(6)} %sub.770, f32[]{:T(128)S(6)} %mul.360, f32[]{:T(128)S(6)} %sub.767, f32[]{:T(128)S(6)} %mul.357, f32[]{:T(128)S(6)} %sub.764, f32[]{:T(128)S(6)} %mul.354, ...), kind=kOutput, calls=%fused_computation.50 | convolution fusion | flops 32243712 | bytes 811132 | tf_op jit(solution)/shard_map/dot_general | solution.py:38
  209.1 1.7 constant_dynamic-update-slice_fusion.1
  210.7 3.2 fusion.2
  213.9 78.0 %all-reduce.15.cloned.1.call-done = (f32[2048,128]{0,1:T(8,128)}, f32[128,7168]{1,0:T(8,128)}) async-done(((f32[2048,128]{0,1:T(8,128)}, f32[128,7168]{1,0:T(8,128)}), (f32[2048,128]{0,1:T(8,128)}, f32[128,7168]{1,0:T(8,128)})) %all-reduce.15.cloned.1.call-update) | async-done | bytes 4718608 | tf_op jit(solution)/shard_map/psum | solution.py:17
  291.9 2.9 dynamic-slice_select_fusion
  294.9 28.9 %convolution_subtract_fusion.1 = f32[2048,3584]{0,1:T(8,128)} fusion(f32[2048,3584]{0,1:T(8,128)} %fusion.2, f32[2048,128]{0,1:T(8,128)S(1)} %copy-done.2, f32[128,3584]{1,0:T(8,128)S(1)} %copy-done, pred[3584]{0:T(1024)(128)(4,1)S(1)} %fusion.47), kind=kOutput, calls=%fused_computation.1 | convolution fusion | flops 11282087936 | bytes 61607424 | tf_op jit(solution)/shard_map/dot_general | solution.py:80
  323.8 3.1 fusion.20
  326.9 45.7 %all-reduce.11.cloned.1.call-done = f32[128,3584]{1,0:T(8,128)} async-done(((f32[128,3584]{1,0:T(8,128)}), f32[128,3584]{1,0:T(8,128)}) %all-reduce.11.cloned.1.call-update) | async-done | bytes 1835024 | tf_op jit(solution)/shard_map/psum | solution.py:17
  372.6 2.3 convolution_subtract_fusion.5
  374.9 3.2 fusion.10
  378.1 2.1 fusion.18
  381.3 2.3 fusion.9
  383.7 2.0 fusion.16
  386.7 2.3 fusion.8
  389.1 2.0 fusion.14
  393.4 1.7 constant_dynamic-update-slice_fusion
  395.1 2.9 fusion.3
  398.0 48.8 %all-reduce.13.cloned.1.call-done = f32[2048,128]{0,1:T(8,128)} async-done(((f32[2048,128]{0,1:T(8,128)}), f32[2048,128]{0,1:T(8,128)}) %all-reduce.13.cloned.1.call-update) | async-done | bytes 1048592 | tf_op jit(solution)/shard_map/psum | solution.py:17
  446.8 30.3 %convolution_subtract_fusion = f32[2048,3584]{0,1:T(8,128)} fusion(f32[2048,3584]{0,1:T(8,128)} %fusion.3, f32[2048,128]{0,1:T(8,128)} %all-reduce.13.cloned.1.call-done, f32[128,3584]{1,0:T(8,128)S(1)} %copy-done.1, pred[3584]{0:T(1024)(128)(4,1)S(1)} %fusion.46), kind=kOutput, calls=%fused_computation | convolution fusion | flops 11282087936 | bytes 61607424 | tf_op jit(solution)/shard_map/dot_general | solution.py:80
  477.1 27.6 %copy.13 = f32[2048,3584]{1,0:T(8,128)} copy(f32[2048,3584]{0,1:T(8,128)} %convolution_subtract_fusion) | data formatting | bytes 58720256 | tf_op jit(solution)/shard_map/sub | solution.py:80
  (47 shorter events, 13.1 us)
Async XLA Ops:
  6.5 86.5 %all-reduce.7.cloned.1.call-start = ((), (), s32[]{:S(2)}) async-start(), calls=%async_computation | async-start | bytes 7340032 | tf_op jit(solution)/shard_map/psum | solution.py:17
  17.6 78.4 %copy-start.7 = (s32[16]{0:T(128)S(1)}, s32[16]{0:T(128)}, u32[]{:S(2)}) copy-start(s32[16]{0:T(128)} %param.30) | copy-start | bytes 196
  17.6 156.1 %all-reduce.9.cloned.1.call-start = ((), (), s32[]{:S(2)}) async-start(), calls=%async_computation.1 | async-start | bytes 3670016 | tf_op jit(solution)/shard_map/psum | solution.py:17
  96.0 195.9 %all-reduce.15.cloned.1.call-start = ((), (), s32[]{:S(2)}) async-start(), calls=%async_computation.4 | async-start | bytes 9437184 | tf_op jit(solution)/shard_map/psum | solution.py:17
  135.0 31.4 %copy-start.3 = (f32[2,128,128]{2,1,0:T(8,128)S(1)}, f32[2,128,128]{2,1,0:T(8,128)}, u32[]{:S(2)}) copy-start(f32[2,128,128]{2,1,0:T(8,128)} %param.29) | copy-start | bytes 393220
  135.1 31.4 %copy-start.4 = (f32[2048]{0:T(1024)S(1)}, f32[2048]{0:T(1024)}, u32[]{:S(2)}) copy-start(f32[2048]{0:T(1024)} %param.27) | copy-start | bytes 24580
  179.3 2.2 copy-start
  186.9 3.4 copy-start.5
  206.0 3.1 copy-start.6
  206.0 166.6 %all-reduce.11.cloned.1.call-start = ((), (), s32[]{:S(2)}) async-start(), calls=%async_computation.2 | async-start | bytes 3670016 | tf_op jit(solution)/shard_map/psum | solution.py:17
  291.9 3.0 copy-start.2
  294.9 151.9 %all-reduce.13.cloned.1.call-start = ((), (), s32[]{:S(2)}) async-start(), calls=%async_computation.3 | async-start | bytes 2097152 | tf_op jit(solution)/shard_map/psum | solution.py:17
  378.1 2.2 copy-start.1
Sparse Core Ops, SparseCore 0:
  17.8 75.2 all-reduce.6
  96.1 77.5 all-reduce.8
  206.1 85.7 all-reduce.14
  295.0 77.5 all-reduce.10
  392.3 54.4 all-reduce.12
where the time goes:
time: 521 us; the launch traced here: 512 us
  waiting for transfers between devices  252 us (48%)
  matrix products  101 us (19%)
  local copies, waits for them, and re-layouts  59.6 us (11%)
  between operations  57.1 us (11%)
  other arithmetic  41.5 us (8%)
    psum x5, waiting for transfers between devices, from_root(): return lax.psum(kept, axis)  252 us
    dot_general x2, matrix products, local(): jnp.dot(errors, trail_rows, precision=lax.Precision.HIGHEST, preferred_el...  59.1 us
    dot_general x8, matrix products, inner_block(): jnp.dot(current - quantized, inverse[low_col:low_col + SUB, low_col:low_c...  31 us
    unnamed x17, local copies, waits for them, and re-layouts  30 us
    sub x1, local copies, waits for them, and re-layouts, local(): weight - jnp.dot(errors, trail_rows, precision=lax.Precision.HIGHEST, pre...  27.6 us
    scatter x8, other arithmetic, inner_block(): block_cols = block_cols.at[:, low_col:low_col + SUB].set(quantized)  19.2 us
    select_n x5, other arithmetic, from_root(): jnp.where(lax.axis_index(axis) == source, value, 0).astype(value.dtype)  14 us
    dot_general x8, matrix products, inner_block(): jnp.dot(error_part, later_rows, precision=lax.Precision.HIGHEST, preferre...  11 us
  transfers between devices with their start and end apart: 5, of which 5 were waited for; matrix products, arithmetic and copies ran while one was open for 16% of the time, Pallas kernels for 0%

commit v1 on v0

v1 whole, which is shorter than its diff:
```python
import functools

import jax
import jax.numpy as jnp
from jax import lax
from jax.experimental import pallas as pl
from jax.experimental.pallas import tpu as pltpu
from jax.sharding import PartitionSpec as P

BLK = 128
SUB = 32
LEVELS = 16
BLOCKS = 2
GROUPS = BLK // SUB

softness = 0.2
F32, BF16 = jnp.float32, jnp.bfloat16


def split2(x):
    hi = x.astype(BF16)
    return hi, (x - hi.astype(F32)).astype(BF16)


def split3(x):
    hi = x.astype(BF16)
    rest = x - hi.astype(F32)
    mid = rest.astype(BF16)
    return hi, mid, (rest - mid.astype(F32)).astype(BF16)


def rounding_rows(inverse, diag_block):
    rows = lax.broadcasted_iota(jnp.int32, (BLK, BLK), 0) // SUB
    cols = lax.broadcasted_iota(jnp.int32, (BLK, BLK), 1) // SUB
    inv = jnp.where(rows == cols, inverse, 0.0)
    later = jnp.where(cols > rows, diag_block, 0.0)
    return inv + jnp.dot(
        inv, later, precision=lax.Precision.HIGHEST, preferred_element_type=F32
    )


def inner_block(block_t, scale, codes_ref, g_ref, base):
    levels = [codes_ref[k].astype(F32) for k in range(LEVELS)]
    sharp = 0.5 / softness
    center = 0.5 * (levels[0] + levels[LEVELS - 1])
    half = [0.5 * (levels[k + 1] - levels[k]) for k in range(LEVELS - 1)]
    mids = [sharp * 0.5 * (levels[k] + levels[k + 1]) for k in range(LEVELS - 1)]
    gain = sharp / scale
    groups = [block_t[j * SUB : (j + 1) * SUB, :] for j in range(GROUPS)]
    errors = []
    for j in range(GROUPS):
        current = groups[j]
        ratio = current * gain
        total = jnp.zeros_like(current) + center
        for k in range(LEVELS - 1):
            total = total + half[k] * jnp.tanh(ratio - mids[k])
        quantized = total * scale
        h, m, l = split3(current - quantized)
        stacked = jnp.concatenate([h, m, h, l, h, m, l, m], axis=0)
        moved = jnp.dot(g_ref[base + j], stacked, preferred_element_type=F32)
        errors.append(moved[j * SUB : (j + 1) * SUB, :])
        for i in range(j + 1, GROUPS):
            groups[i] = groups[i] - moved[i * SUB : (i + 1) * SUB, :]
        groups[j] = quantized
    return jnp.concatenate(groups, axis=0), jnp.concatenate(errors, axis=0)


def round_kernel(
    chunk, meta_ref, codes_ref, inv_ref, diag_ref, p0_ref, p1_ref, scale_ref, wblk_ref, w_ref, out_ref,
    pcat, gcat, ecat, block
):
    step = pl.program_id(0)
    cols_per = w_ref.shape[1]
    first = meta_ref[0]
    cut0, cut1 = meta_ref[1] + BLK, meta_ref[2] + BLK
    is_first = first == meta_ref[1]
    is_last = first == meta_ref[2]

    @pl.when(step == 0)
    def _():
        @pl.loop(0, cols_per // chunk)
        def _(i):
            at = pl.ds(pl.multiple_of(i * chunk, chunk), chunk)
            ids = first + i * chunk + lax.broadcasted_iota(jnp.int32, (BLK, chunk), 1)
            for b, (p_ref, cut) in enumerate(((p0_ref, cut0), (p1_ref, cut1))):
                hi, lo = split2(jnp.where(ids >= cut, p_ref[:, at], 0.0))
                pcat[b * BLK : (b + 1) * BLK, at] = hi
                pcat[(2 + b) * BLK : (3 + b) * BLK, at] = lo
                pcat[(4 + b) * BLK : (5 + b) * BLK, at] = hi

        for b in range(BLOCKS):
            diag = diag_ref[...] if b == 0 else p1_ref[:, :BLK]
            pieces = split3(rounding_rows(inv_ref[b], diag))
            h, m, l = [piece.astype(F32) for piece in pieces]
            for j in range(GROUPS):
                at = slice(j * SUB, (j + 1) * SUB)
                stacked = jnp.concatenate(
                    [h[at], h[at], m[at], h[at], l[at], m[at], m[at], l[at]], axis=0
                )
                gcat[b * GROUPS + j] = stacked.T.astype(BF16)
        ecat[...] = jnp.zeros_like(ecat)

    def put_errors(b, errors_t):
        hi, lo = split2(errors_t.T)
        ecat[:, b * BLK : (b + 1) * BLK] = hi
        ecat[:, (2 + b) * BLK : (3 + b) * BLK] = hi
        ecat[:, (4 + b) * BLK : (5 + b) * BLK] = lo

    scale = scale_ref[...]
    rounded, errors = inner_block(wblk_ref[...].T, scale, codes_ref, gcat, 0)
    put_errors(0, errors)
    block[...] = rounded

    @pl.when(is_last)
    def _():
        change = jnp.zeros((w_ref.shape[0], BLK), F32)
        for k in (0, 2, 4):
            at = slice(k * BLK, (k + 1) * BLK)
            change += jnp.dot(ecat[:, at], pcat[at, :BLK], preferred_element_type=F32)
        current = w_ref[:, :BLK] - change
        rounded, errors = inner_block(current.T, scale, codes_ref, gcat, GROUPS)
        put_errors(1, errors)
        block[...] = rounded

    @pl.loop(0, cols_per // chunk)
    def _(i):
        at = pl.ds(pl.multiple_of(i * chunk, chunk), chunk)
        out_ref[:, at] = w_ref[:, at] - jnp.dot(
            ecat[...], pcat[:, at], preferred_element_type=F32
        )

    @pl.when(jnp.logical_or(is_first, is_last))
    def _():
        out_ref[:, :BLK] = block[...].T


def round_local(meta, grid_codes, block_inverse, diag, p0, p1, scales, wblk, weight):
    rows, cols_per = weight.shape
    tile = next(t for t in (512, 256, 128, 64, 32, 16, 8) if rows % t == 0)
    chunk = next(c for c in (512, 256, 128) if cols_per % c == 0)
    smem = pl.BlockSpec(memory_space=pltpu.SMEM)

    def whole(shape):
        return pl.BlockSpec(shape, lambda i: (0,) * len(shape))

    return pl.pallas_call(
        functools.partial(round_kernel, chunk),
        grid=(rows // tile,),
        out_shape=jax.ShapeDtypeStruct(weight.shape, F32),
        in_specs=[
            smem,
            smem,
            whole((BLOCKS, BLK, BLK)),
            whole((BLK, BLK)),
            whole((BLK, cols_per)),
            whole((BLK, cols_per)),
            pl.BlockSpec((1, tile), lambda i: (0, i)),
            pl.BlockSpec((tile, BLK), lambda i: (i, 0)),
            pl.BlockSpec((tile, cols_per), lambda i: (i, 0)),
        ],
        out_specs=pl.BlockSpec((tile, cols_per), lambda i: (i, 0)),
        scratch_shapes=[
            pltpu.VMEM((6 * BLK, cols_per), BF16),
            pltpu.VMEM((BLOCKS * GROUPS, BLK, 8 * SUB), BF16),
            pltpu.VMEM((tile, 6 * BLK), BF16),
            pltpu.VMEM((BLK, tile), F32),
        ],
        compiler_params=pltpu.CompilerParams(
            dimension_semantics=("arbitrary",), vmem_limit_bytes=60 * 1024 * 1024
        ),
        name="round_local",
    )(meta, grid_codes, block_inverse, diag, p0, p1, scales[None, :], wblk, weight)


def local(weight, scales, panels, block_inverse, grid_codes, block_starts):
    cols_per = weight.shape[1]
    slab_width = panels.shape[1]
    own, row = lax.axis_index("cols"), lax.axis_index("rows")
    first = own * cols_per
    holder = first // slab_width
    offset = first - holder * slab_width
    start0, start1 = block_starts[0], block_starts[1]
    mine = own == start0 // cols_per
    slab, wblk = lax.psum(
        (jnp.where(mine, panels, 0.0), jnp.where(mine, weight[:, :BLK], 0.0)), "cols"
    )
    both = jnp.concatenate([slab, panels], axis=0)
    needed = lax.dynamic_slice_in_dim(both, offset, cols_per, 1)
    diag = lax.dynamic_slice_in_dim(slab, start0 % slab_width, BLK, 1)
    needed, diag = lax.psum(
        (jnp.where(row == holder, needed, 0.0), jnp.where(row == start0 // slab_width, diag, 0.0)), "rows"
    )
    meta = jnp.stack([first, start0, start1]).astype(jnp.int32)
    return round_local(
        meta, grid_codes, block_inverse, diag, needed[:BLK], needed[BLK:], scales, wblk, weight
    )


def solution(mesh):
    placed = (P("rows", "cols"), P("rows"), P("cols", "rows"), P(), P(), P())
    return jax.shard_map(
        local, mesh=mesh, in_specs=placed, out_specs=P("rows", "cols"), check_vma=False
    )
```

time: 521 us -> 297 us (0.57); the launches traced: 512 us -> 296 us
  matrix products: 101 us -> 0 us
  local copies, waits for them, and re-layouts: 59.6 us -> 4.68 us
  between operations: 57.1 us -> 15.5 us
  Pallas kernels: 0 us -> 38 us
  other arithmetic: 41.5 us -> 10.9 us
  waiting for transfers between devices: 252 us -> 227 us
    dot_general x18 -> x0, matrix products: 101 us -> none  [the longest x2 59.1 us: local(): jnp.dot(errors, trail_rows, precision=lax.Precision.HIGHEST, preferred_el...]
    pallas_call x0 -> x1, Pallas kernels: none -> 38 us  [round_local(): pl.pallas_call(functools.partial(round_kernel, chunk), grid=(rows // tile...]
    unnamed x17 -> x2, local copies, waits for them, and re-layouts: 30 us -> 0.55 us
    sub x1 -> x0, local copies, waits for them, and re-layouts: 27.6 us -> none  [local(): weight - jnp.dot(errors, trail_rows, precision=lax.Precision.HIGHEST, pre...]
    psum x5 -> x2, waiting for transfers between devices: 252 us -> 227 us  [the longest x1 141 us: local(): lax.psum((jnp.where(row == holder, needed, 0.0), jnp.where(row == start0...]
    scatter x8 -> x0, other arithmetic: 19.2 us -> none  [inner_block(): block_cols = block_cols.at[:, low_col:low_col + SUB].set(quantized)]
    select_n x7 -> x4, other arithmetic: 20.1 us -> 10.2 us  [the longest x1 4.13 us: local(): jnp.where(row == holder, needed, 0.0)]
  transfers between devices with their start and end apart: 5 -> 2, of which waited for: 5 -> 2; matrix products, arithmetic and copies ran while one was open for 16% -> 0% of each run, Pallas kernels for 0% -> 0%
where the time goes in v1:
time: 297 us; the launch traced here: 296 us
  waiting for transfers between devices  227 us (76%)
  Pallas kernels  38 us (13%)
  between operations  15.5 us (5%)
  other arithmetic  10.9 us (4%)
  local copies, waits for them, and re-layouts  4.68 us (2%)
    psum x1, waiting for transfers between devices, local(): lax.psum((jnp.where(row == holder, needed, 0.0), jnp.where(row == start0...  141 us
    psum x1, waiting for transfers between devices, local(): lax.psum((jnp.where(mine, panels, 0.0), jnp.where(mine, weight[:, :BLK],...  86.4 us
    pallas_call x1, Pallas kernels, round_local(): pl.pallas_call(functools.partial(round_kernel, chunk), grid=(rows // tile...  38 us
  transfers between devices with their start and end apart: 2, of which 2 were waited for; matrix products, arithmetic and copies ran while one was open for 0% of the time, Pallas kernels for 0%

profile of v1, /device:TPU:7, one launch (start us, length us, event | category | flops | bytes accessed | tf_op | source)
XLA Modules:
  0.0 296.1 jit_solution(17287176778325516469)
XLA Ops:
  6.5 0.0 all-reduce.5.cloned.1.call-start
  8.5 2.3 slice_select_fusion
  10.8 2.2 broadcast_select_fusion
  13.0 0.0 copy-start
  13.0 0.0 all-reduce.5.cloned.1.call-update
  13.0 0.0 all-reduce.7.cloned.1.call-start
  13.1 0.5 copy-done
  13.8 86.4 %all-reduce.5.cloned.1.call-done = (f32[128,7168]{1,0:T(8,128)}, f32[2048,128]{1,0:T(8,128)}) async-done(((f32[128,7168]{1,0:T(8,128)}, f32[2048,128]{1,0:T(8,128)}), (f32[128,7168]{1,0:T(8,128)}, f32[2048,128]{1,0:T(8,128)})) %all-reduce.5.cloned.1.call-update) | async-done | bytes 4718608 | tf_op jit(solution)/shard_map/psum | solution.py:184
  100.2 1.6 dynamic-slice_select_fusion
  101.8 4.1 %fusion.1 = f32[256,3584]{1,0:T(8,128)} fusion(s32[]{:T(128)S(6)} %select_n.65, f32[128,7168]{1,0:T(8,128)} %get-tuple-element.5, f32[128,7168]{1,0:T(8,128)} %param.8, pred[]{:T(512)S(6)} %eq.13), kind=kLoop, calls=%fused_computation.3 | loop fusion | flops 1835008 | bytes 11010053 | tf_op jit(solution)/shard_map/jit(_where)/select_n | solution.py:191
  105.9 0.0 all-reduce.7.cloned.1.call-update
  106.0 0.6 pad_add_fusion.meta_ref
  106.6 140.5 %all-reduce.7.cloned.1.call-done = (f32[128,128]{1,0:T(8,128)}, f32[256,3584]{1,0:T(8,128)}) async-done(((f32[128,128]{1,0:T(8,128)}, f32[256,3584]{1,0:T(8,128)}), (f32[128,128]{1,0:T(8,128)}, f32[256,3584]{1,0:T(8,128)})) %all-reduce.7.cloned.1.call-update) | async-done | bytes 3735568 | tf_op jit(solution)/shard_map/psum | solution.py:190
  247.1 4.1 %fusion.2 = (f32[128,3584]{1,0:T(8,128)}, f32[128,3584]{1,0:T(8,128)}) fusion(f32[256,3584]{1,0:T(8,128)} %get-tuple-element.8), kind=kLoop, calls=%fused_computation.8 | loop fusion | bytes 7340032 | tf_op jit(solution)/shard_map/slice | solution.py:195
  251.2 38.0 %round_local.1 = f32[2048,3584]{1,0:T(8,128)} custom-call(s32[3]{0:T(128)} %pad_add_fusion.meta_ref, s32[16]{0:T(128)} %codes_ref.1, f32[2,128,128]{2,1,0:T(8,128)} %inv_ref.1, f32[128,128]{1,0:T(8,128)} %get-tuple-element.7.diag_ref, f32[128,3584]{1,0:T(8,128)} %get-tuple-element.10.p0_ref, f32[128,3584]{1,0:T(8,128)} %get-tuple-element.9.p1_ref, ...), custom_call_target="tpu_custom_call" | custom-call | tf_op jit(solution)/shard_map/round_local/pallas_call | solution.py:146
Async XLA Ops:
  6.5 93.6 %all-reduce.5.cloned.1.call-start = ((), (), s32[]{:S(2)}) async-start(), calls=%async_computation | async-start | bytes 9437184 | tf_op jit(solution)/shard_map/psum | solution.py:184
  13.0 0.7 copy-start
  13.0 234.1 %all-reduce.7.cloned.1.call-start = ((), (), s32[]{:S(2)}) async-start(), calls=%async_computation.1 | async-start | bytes 7471104 | tf_op jit(solution)/shard_map/psum | solution.py:190
Sparse Core Ops, SparseCore 0:
  13.1 87.0 all-reduce.4
  106.1 140.9 all-reduce.6

commit v2 on v1

--- a/solution.py
+++ b/solution.py
@@ -15,6 +15,7 @@
 
 softness = 0.2
 F32, BF16 = jnp.float32, jnp.bfloat16
+MESH = pl.DeviceIdType.MESH
 
 
 def split2(x):
@@ -172,28 +173,163 @@
     )(meta, grid_codes, block_inverse, diag, p0, p1, scales[None, :], wblk, weight)
 
 
+def spread_kernel(
+    pieces, ratio, last_only, with_diag, x_ref, d_ref, out_ref, dout_ref,
+    held, slots, recv_sem, up_sem, down_sem, dsend_sem, drecv_sem
+):
+    rows, cols = lax.axis_size("rows"), lax.axis_size("cols")
+    me, col = lax.axis_index("rows"), lax.axis_index("cols")
+    holder = col // ratio
+    depth = x_ref.shape[0] // pieces
+
+    barrier = pltpu.get_barrier_semaphore()
+    for step in range(1, rows):
+        other = lax.rem(me + step, rows)
+        pl.semaphore_signal(barrier, inc=1, device_id=(col, other), device_id_type=MESH)
+    pl.semaphore_wait(barrier, rows - 1)
+
+    def part(ref, i):
+        return ref.at[pl.ds(i * depth, depth)]
+
+    def copy(source, i, sems, target):
+        return pltpu.make_async_remote_copy(
+            src_ref=part(source, i),
+            dst_ref=part(held, i),
+            send_sem=sems.at[i],
+            recv_sem=recv_sem.at[i],
+            device_id=(col, target),
+            device_id_type=MESH,
+        )
+
+    def diag_copy(step):
+        other = lax.rem(me + step, rows)
+        return pltpu.make_async_remote_copy(
+            src_ref=d_ref,
+            dst_ref=slots.at[step - 1],
+            send_sem=dsend_sem.at[step - 1],
+            recv_sem=drecv_sem.at[step - 1],
+            device_id=(col, other),
+            device_id_type=MESH,
+        )
+
+    if with_diag:
+        for step in range(1, rows):
+            diag_copy(step).start()
+
+    active = col == cols - 1 if last_only else col >= 0
+    goes_up = jnp.logical_and(me >= holder, me < rows - 1)
+    goes_down = jnp.logical_and(me <= holder, me > 0)
+    up = lax.rem(me + 1, rows)
+    down = lax.rem(me + rows - 1, rows)
+
+    @pl.when(active)
+    def _():
+        @pl.when(me == holder)
+        def _():
+            for i in range(pieces):
+                @pl.when(goes_up)
+                def _():
+                    copy(x_ref, i, up_sem, up).start()
+
+                @pl.when(goes_down)
+                def _():
+                    copy(x_ref, i, down_sem, down).start()
+
+            out_ref[...] = x_ref[...]
+
+        @pl.when(me != holder)
+        def _():
+            for i in range(pieces):
+                copy(held, i, up_sem, up).wait_recv()
+
+                @pl.when(goes_up)
+                def _():
+                    copy(held, i, up_sem, up).start()
+
+                @pl.when(goes_down)
+                def _():
+                    copy(held, i, down_sem, down).start()
+
+                at = slice(i * depth, (i + 1) * depth)
+                out_ref[at, :] = held[at, :]
+
+        for i in range(pieces):
+            @pl.when(goes_up)
+            def _():
+                copy(held, i, up_sem, up).wait_send()
+
+            @pl.when(goes_down)
+            def _():
+                copy(held, i, down_sem, down).wait_send()
+
+    if last_only:
+        @pl.when(jnp.logical_not(active))
+        def _():
+            out_ref[...] = x_ref[...]
+
+    if with_diag:
+        total = d_ref[...]
+        for step in range(1, rows):
+            diag_copy(step).wait()
+            total = total + slots[step - 1]
+        dout_ref[...] = total
+    else:
+        dout_ref[...] = d_ref[...]
+
+
+def spread(x, diag, ratio, last_only, with_diag, collective_id):
+    rows = lax.axis_size("rows")
+    pieces = 16
+    vmem = pl.BlockSpec(memory_space=pltpu.VMEM)
+    sems = pltpu.SemaphoreType.DMA
+    return pl.pallas_call(
+        functools.partial(spread_kernel, pieces, ratio, last_only, with_diag),
+        out_shape=(
+            jax.ShapeDtypeStruct(x.shape, F32),
+            jax.ShapeDtypeStruct(diag.shape, F32),
+        ),
+        in_specs=[vmem, vmem],
+        out_specs=(vmem, vmem),
+        scratch_shapes=[
+            pltpu.VMEM(x.shape, F32),
+            pltpu.VMEM((rows - 1,) + diag.shape, F32),
+            sems((pieces,)),
+            sems((pieces,)),
+            sems((pieces,)),
+            sems((rows - 1,)),
+            sems((rows - 1,)),
+        ],
+        compiler_params=pltpu.CompilerParams(
+            collective_id=collective_id, has_side_effects=True
+        ),
+        cost_estimate=pl.CostEstimate(
+            flops=0, bytes_accessed=64 * x.size * 4, transcendentals=0
+        ),
+        name="spread",
+    )(x, diag)
+
+
 def local(weight, scales, panels, block_inverse, grid_codes, block_starts):
     cols_per = weight.shape[1]
     slab_width = panels.shape[1]
     own, row = lax.axis_index("cols"), lax.axis_index("rows")
     first = own * cols_per
-    holder = first // slab_width
-    offset = first - holder * slab_width
+    ratio = slab_width // cols_per
+    offset = first % slab_width
     start0, start1 = block_starts[0], block_starts[1]
     mine = own == start0 // cols_per
     slab, wblk = lax.psum(
         (jnp.where(mine, panels, 0.0), jnp.where(mine, weight[:, :BLK], 0.0)), "cols"
     )
-    both = jnp.concatenate([slab, panels], axis=0)
-    needed = lax.dynamic_slice_in_dim(both, offset, cols_per, 1)
+    none = jnp.zeros((8, BLK), F32)
+    own1 = lax.dynamic_slice_in_dim(panels, offset, cols_per, 1)
+    p1, _ = spread(own1, none, ratio, True, False, 1)
+    own0 = lax.dynamic_slice_in_dim(slab, offset, cols_per, 1)
     diag = lax.dynamic_slice_in_dim(slab, start0 % slab_width, BLK, 1)
-    needed, diag = lax.psum(
-        (jnp.where(row == holder, needed, 0.0), jnp.where(row == start0 // slab_width, diag, 0.0)), "rows"
-    )
+    diag = jnp.where(row == start0 // slab_width, diag, 0.0)
+    p0, diag = spread(own0, diag, ratio, False, True, 2)
     meta = jnp.stack([first, start0, start1]).astype(jnp.int32)
-    return round_local(
-        meta, grid_codes, block_inverse, diag, needed[:BLK], needed[BLK:], scales, wblk, weight
-    )
+    return round_local(meta, grid_codes, block_inverse, diag, p0, p1, scales, wblk, weight)
 
 
 def solution(mesh):

time: 297 us -> 207 us (0.70)
  waiting for transfers between devices: 227 us -> 49.8 us
  Pallas kernels: 38 us -> 127 us
  other arithmetic: 10.9 us -> 6.74 us
  local copies, waits for them, and re-layouts: 4.68 us -> 7.78 us
    psum x1 -> x0, waiting for transfers between devices: 141 us -> none  [local(): lax.psum((jnp.where(row == holder, needed, 0.0), jnp.where(row == start0...]
    pallas_call x0 -> x2, Pallas kernels: none -> 89.4 us  [spread(): pl.pallas_call(functools.partial(spread_kernel, pieces, ratio, last_only,...]
    psum x1, waiting for transfers between devices: 86.4 us -> 49.8 us  [local(): lax.psum((jnp.where(mine, panels, 0.0), jnp.where(mine, weight[:, :BLK],...]
    dynamic_slice x0 -> x2, local copies, waits for them, and re-layouts: none -> 6.58 us  [the longest x1 3.31 us: local(): own1 = lax.dynamic_slice_in_dim(panels, offset, cols_per, 1)]
    slice x1 -> x0, local copies, waits for them, and re-layouts: 4.14 us -> none  [local(): needed[BLK:]]
    select_n x2 -> x1, other arithmetic: 5.75 us -> 1.62 us  [local(): diag = jnp.where(row == start0 // slab_width, diag, 0.0)]
  transfers between devices with their start and end apart: 2 -> 1, of which waited for: 2 -> 1; matrix products, arithmetic and copies ran while one was open for 0% -> 2% of each run, Pallas kernels for 0% -> 16%
where the time goes in v2:
time: 207 us
  Pallas kernels  127 us (61%)
  waiting for transfers between devices  49.8 us (24%)
  between operations  15.5 us (7%)
  local copies, waits for them, and re-layouts  7.78 us (4%)
  other arithmetic  6.74 us (3%)
    pallas_call x2, Pallas kernels, spread(): pl.pallas_call(functools.partial(spread_kernel, pieces, ratio, last_only,...  89.4 us
    psum x1, waiting for transfers between devices, local(): lax.psum((jnp.where(mine, panels, 0.0), jnp.where(mine, weight[:, :BLK],...  49.8 us
    pallas_call x1, Pallas kernels, round_local(): pl.pallas_call(functools.partial(round_kernel, chunk), grid=(rows // tile...  38 us
  transfers between devices with their start and end apart: 1, of which 1 were waited for; matrix products, arithmetic and copies ran while one was open for 2% of the time, Pallas kernels for 16%

profile of v2, /device:TPU:7, one launch (start us, length us, event | category | flops | bytes accessed | tf_op | source)
XLA Modules:
  0.0 207.3 jit_solution(9004958407224225533)
XLA Ops:
  6.5 0.0 all-reduce.3.cloned.1.call-start
  8.5 2.3 %slice_select_fusion = f32[2048,128]{1,0:T(8,128)} fusion(f32[2048,3584]{1,0:T(8,128)} %w_ref.1, pred[]{:T(512)S(6)} %eq.9), kind=kLoop, calls=%fused_computation.1 | loop fusion | flops 262144 | bytes 2097153 | tf_op jit(solution)/shard_map/jit(_where)/select_n | solution.py:322
  10.8 2.2 %broadcast_select_fusion = f32[128,7168]{1,0:T(8,128)} fusion(f32[128,7168]{1,0:T(8,128)} %param.8, pred[]{:T(512)S(6)} %eq.9), kind=kLoop, calls=%fused_computation | loop fusion | flops 917504 | bytes 7340033 | tf_op jit(solution)/shard_map/jit(_where)/select_n | solution.py:322
  13.0 0.0 copy-start
  13.0 0.0 all-reduce.3.cloned.1.call-update
  13.1 0.6 copy-done
  13.8 3.3 %constant_dynamic-slice_fusion.x_ref = f32[128,3584]{1,0:T(8,128)} fusion(f32[128,7168]{1,0:T(8,128)} %param.8, s32[]{:T(128)S(6)} %select_n.53), kind=kLoop, calls=%fused_computation.3 | loop fusion | bytes 3670020 | tf_op jit(solution)/shard_map/dynamic_slice | solution.py:325
  17.1 0.6 broadcast_in_dim.20.d_ref
  17.7 33.1 %spread.3 = (f32[128,3584]{1,0:T(8,128)}, f32[8,128]{1,0:T(8,128)}) custom-call(f32[128,3584]{1,0:T(8,128)} %constant_dynamic-slice_fusion.x_ref, f32[8,128]{1,0:T(8,128)} %broadcast_in_dim.20.d_ref), custom_call_target="tpu_custom_call" | custom-call | bytes 117440512 | tf_op jit(solution)/shard_map/spread/pallas_call | solution.py:285
  50.8 0.6 pad_add_fusion.meta_ref
  51.4 49.8 %all-reduce.3.cloned.1.call-done = (f32[128,7168]{1,0:T(8,128)}, f32[2048,128]{1,0:T(8,128)}) async-done(((f32[128,7168]{1,0:T(8,128)}, f32[2048,128]{1,0:T(8,128)}), (f32[128,7168]{1,0:T(8,128)}, f32[2048,128]{1,0:T(8,128)})) %all-reduce.3.cloned.1.call-update) | async-done | bytes 4718608 | tf_op jit(solution)/shard_map/psum | solution.py:321
  101.2 3.3 %constant_dynamic-slice_fusion.1.x_ref = f32[128,3584]{1,0:T(8,128)} fusion(f32[128,7168]{1,0:T(8,128)} %get-tuple-element.11, s32[]{:T(128)S(6)} %select_n.53), kind=kLoop, calls=%fused_computation.4 | loop fusion | bytes 3670020 | tf_op jit(solution)/shard_map/dynamic_slice | solution.py:327
  104.5 1.6 dynamic-slice_select_fusion.d_ref
  106.1 56.3 %spread.2 = (f32[128,3584]{1,0:T(8,128)}, f32[128,128]{1,0:T(8,128)}) custom-call(f32[128,3584]{1,0:T(8,128)} %constant_dynamic-slice_fusion.1.x_ref, f32[128,128]{1,0:T(8,128)} %dynamic-slice_select_fusion.d_ref), custom_call_target="tpu_custom_call" | custom-call | bytes 117440512 | tf_op jit(solution)/shard_map/spread/pallas_call | solution.py:285
  162.4 38.0 %round_local.1 = f32[2048,3584]{1,0:T(8,128)} custom-call(s32[3]{0:T(128)} %pad_add_fusion.meta_ref, s32[16]{0:T(128)} %codes_ref.1, f32[2,128,128]{2,1,0:T(8,128)} %inv_ref.1, f32[128,128]{1,0:T(8,128)} %get-tuple-element.8.diag_ref, f32[128,3584]{1,0:T(8,128)} %get-tuple-element.9.p0_ref, f32[128,3584]{1,0:T(8,128)} %get-tuple-element.10.p1_ref, ...), custom_call_target="tpu_custom_call" | custom-call | tf_op jit(solution)/shard_map/round_local/pallas_call | solution.py:147
Async XLA Ops:
  6.5 94.7 %all-reduce.3.cloned.1.call-start = ((), (), s32[]{:S(2)}) async-start(), calls=%async_computation | async-start | bytes 9437184 | tf_op jit(solution)/shard_map/psum | solution.py:321
  13.0 0.7 copy-start
Sparse Core Ops, SparseCore 0:
  13.2 87.9 all-reduce.2
